TPU v7x, 32 devices: a whole 2x2x4 slice. The times are simulated.
32 devices in a mesh: dp: 8 (over z, x), head: 4 (over y, core).
Axes of the slice: x: 2, y: 2, z: 4, core: 2. Of those that a mesh axis runs over, the one named last changes fastest.
Arguments:
- inputs: bfloat16 [8192, 2048], P('dp'), may hold values from -6 to 6
- lengths: int32 [8], P('dp'), may hold values from 256 to 1024, as said below
- gain_attn: bfloat16 [2048], P('dp'), may hold values from 0.5 to 1.5
- w_query: bfloat16 [2048, 2048], P('dp', 'head'), may hold values from -0.25 to 0.25
- w_key: bfloat16 [2048, 2048], P('dp', 'head'), may hold values from -0.25 to 0.25
- w_value: bfloat16 [2048, 2048], P('dp', 'head'), may hold values from -0.125 to 0.125
- w_slot: bfloat16 [2048, 256], P('dp', 'head'), may hold values from -0.125 to 0.125
- gate_bias: float32 [256], P('head'), may hold values from 0 to 8
- w_out: bfloat16 [2048, 2048], P('head', 'dp'), may hold values from -0.5 to 0.5
- gain_ffn: bfloat16 [2048], P('dp'), may hold values from 0.5 to 1.5
- w_gate: bfloat16 [2048, 5632], P('dp', 'head'), may hold values from -0.125 to 0.125
- w_up: bfloat16 [2048, 5632], P('dp', 'head'), may hold values from -0.125 to 0.125
- w_down: bfloat16 [5632, 2048], P('head', 'dp'), may hold values from -0.078125 to 0.078125
- cotangent: bfloat16 [8192, 2048], P('dp'), may hold values from -6 to 6
Outputs:
- output: bfloat16 [8192, 2048], P('dp')
- grad_inputs: float32 [8192, 2048], P('dp')
- grad_gain_attn: float32 [2048], P('dp')
- grad_w_query: float32 [2048, 2048], P('dp', 'head')
- grad_w_key: float32 [2048, 2048], P('dp', 'head')
- grad_w_value: float32 [2048, 2048], P('dp', 'head')
- grad_w_slot: float32 [2048, 256], P('dp', 'head')
- grad_gate_bias: float32 [256], P('head')
- grad_w_out: float32 [2048, 2048], P('head', 'dp')
- grad_gain_ffn: float32 [2048], P('dp')
- grad_w_gate: float32 [2048, 5632], P('dp', 'head')
- grad_w_up: float32 [2048, 5632], P('dp', 'head')
- grad_w_down: float32 [5632, 2048], P('head', 'dp')
Inputs may be any that keep to these rules, and one draw needn't show every extreme that they name: lengths[s] is the number of valid leading positions of sequence s; some sequence has all 1024 valid.
All inputs are finite; a program needn't handle non-finite values.
Results may differ from a plain program's by a relative error of at most 0.014.
Values may be sent and summed in bfloat16 or wider, within the bound.
A program may use at most 256 MiB of HBM per device.

v0:
```python
import jax
import jax.numpy as jnp
from jax import lax
from jax.sharding import PartitionSpec as P

SPAN = 64
epsilon = 1e-06
damping = 8.0
highest = lax.Precision.HIGHEST


def norm_rows(values, gain):
    factor = lax.rsqrt(jnp.mean(values * values, axis=-1, keepdims=True) + epsilon)
    return values * factor * gain


def swiglu(gate_act, up_act):
    return jax.nn.silu(gate_act) * up_act


def span_step(states, pieces):
    queries, key_rows, value_rows, logdecay, writes = pieces
    state_keys, state_values = states
    rows_count = queries.shape[0]
    cumul = jnp.cumsum(logdecay, axis=0)
    causal = (jnp.arange(rows_count)[:, None] >= jnp.arange(rows_count)[None, :])[:, :, None]
    spread = jnp.where(causal, cumul[:, None, :] - cumul[None, :, :], 0.0)
    weighted = jnp.where(causal, jnp.exp(spread), 0.0) * writes[None, :, :]
    scale_factor = queries.shape[1] ** (-0.5)
    inner_products = jnp.dot(queries, key_rows.T, precision=highest) * scale_factor
    carried = jnp.dot(queries, state_keys.T, precision=highest) * scale_factor
    scores = jnp.exp(cumul) * carried + jnp.einsum(
        "tsj,ts->tj", weighted, inner_products, precision=highest
    )
    slot_probs = jax.nn.softmax(scores, axis=-1)
    mixing = jnp.einsum("tj,tsj->ts", slot_probs, weighted, precision=highest)
    result = jnp.dot(slot_probs * jnp.exp(cumul), state_values, precision=highest) + jnp.dot(
        mixing, value_rows, precision=highest
    )
    last_cumul = cumul[-1]
    tail_weight = jnp.exp(last_cumul[None, :] - cumul) * writes
    new_keys = jnp.exp(last_cumul)[:, None] * state_keys + jnp.dot(
        tail_weight.T, key_rows, precision=highest
    )
    new_values = jnp.exp(last_cumul)[:, None] * state_values + jnp.dot(
        tail_weight.T, value_rows, precision=highest
    )
    return ((new_keys, new_values), result)


def slot_mixer(queries, key_rows, value_rows, gate_logits, valid_mask):
    logdecay = valid_mask[:, None] * jax.nn.log_sigmoid(gate_logits) / damping
    writes = valid_mask[:, None] * (1.0 - jnp.exp(logdecay))
    length = queries.shape[0]
    blocks = length // SPAN

    def blocked(matrix):
        return matrix.reshape(blocks, SPAN, matrix.shape[1])

    start_state = (
        jnp.zeros((gate_logits.shape[1], key_rows.shape[1]), jnp.float32),
        jnp.zeros((gate_logits.shape[1], value_rows.shape[1]), jnp.float32),
    )
    _, outputs = lax.scan(
        jax.checkpoint(span_step),
        start_state,
        (
            blocked(queries),
            blocked(key_rows),
            blocked(value_rows),
            blocked(logdecay),
            blocked(writes),
        ),
    )
    return outputs.reshape(length, value_rows.shape[1]) * valid_mask[:, None]


def matmul_low(left, right):
    return jnp.dot(left, right, preferred_element_type=jnp.float32)


def per_device(
    inputs,
    lengths,
    gain_attn,
    w_query,
    w_key,
    w_value,
    w_slot,
    gate_bias,
    w_out,
    gain_ffn,
    w_gate,
    w_up,
    w_down,
    cotangent,
):
    column_set = (
        lax.all_gather(gain_attn, "dp", axis=0, tiled=True),
        lax.all_gather(gain_ffn, "dp", axis=0, tiled=True),
        lax.all_gather(w_query, "dp", axis=0, tiled=True),
        lax.all_gather(w_key, "dp", axis=0, tiled=True),
        lax.all_gather(w_value, "dp", axis=0, tiled=True),
        lax.all_gather(w_slot, "dp", axis=0, tiled=True),
        lax.all_gather(w_gate, "dp", axis=0, tiled=True),
        lax.all_gather(w_up, "dp", axis=0, tiled=True),
    )
    row_set = (
        lax.all_gather(w_out, "dp", axis=1, tiled=True),
        lax.all_gather(w_down, "dp", axis=1, tiled=True),
    )
    (
        full_gain_attn,
        full_gain_ffn,
        full_query,
        full_key,
        full_value,
        full_slot,
        full_gate,
        full_up,
    ) = column_set
    full_out, full_down = row_set
    rows_in = inputs.astype(jnp.float32)
    length = rows_in.shape[0]
    valid_mask = (jnp.arange(length) < lengths[0]).astype(jnp.float32)
    normed, norm_attn_pull = jax.vjp(norm_rows, rows_in, full_gain_attn.astype(jnp.float32))
    normed_low = normed.astype(jnp.bfloat16)
    queries = matmul_low(normed_low, full_query).astype(jnp.bfloat16)
    key_proj = matmul_low(normed_low, full_key).astype(jnp.bfloat16)
    value_proj = matmul_low(normed_low, full_value).astype(jnp.bfloat16)
    gate_logits = matmul_low(normed_low, full_slot) + gate_bias

    def mixer_local(query_in, key_in, value_in, logit_in):
        return slot_mixer(query_in, key_in, value_in, logit_in, valid_mask)

    mixed, mixer_pull = jax.vjp(
        mixer_local,
        queries.astype(jnp.float32),
        key_proj.astype(jnp.float32),
        value_proj.astype(jnp.float32),
        gate_logits,
    )
    mixed_low = mixed.astype(jnp.bfloat16)
    resid = rows_in + lax.psum(matmul_low(mixed_low, full_out), "head")
    normed2, norm_ffn_pull = jax.vjp(norm_rows, resid, full_gain_ffn.astype(jnp.float32))
    normed2_low = normed2.astype(jnp.bfloat16)
    gate_act = matmul_low(normed2_low, full_gate)
    up_act = matmul_low(normed2_low, full_up)
    hidden, swiglu_pull = jax.vjp(swiglu, gate_act, up_act)
    hidden_low = hidden.astype(jnp.bfloat16)
    output_low = (
        resid
        + lax.psum(matmul_low(hidden_low, full_down).astype(jnp.bfloat16), "head").astype(
            jnp.float32
        )
    ).astype(jnp.bfloat16)
    back_cols = (
        lax.all_gather(w_query, "dp", axis=0, tiled=True),
        lax.all_gather(w_key, "dp", axis=0, tiled=True),
        lax.all_gather(w_value, "dp", axis=0, tiled=True),
        lax.all_gather(w_slot, "dp", axis=0, tiled=True),
        lax.all_gather(w_gate, "dp", axis=0, tiled=True),
        lax.all_gather(w_up, "dp", axis=0, tiled=True),
    )
    back_rows = (
        lax.all_gather(w_out, "dp", axis=1, tiled=True),
        lax.all_gather(w_down, "dp", axis=1, tiled=True),
    )
    full_query, full_key, full_value, full_slot, full_gate, full_up = back_cols
    full_out, full_down = back_rows
    d_hidden = matmul_low(cotangent, full_down.T)
    d_gate, d_up = swiglu_pull(d_hidden)
    d_gate_low = d_gate.astype(jnp.bfloat16)
    d_up_low = d_up.astype(jnp.bfloat16)
    grad_down = matmul_low(hidden_low.T, cotangent)
    grad_gate = matmul_low(normed2_low.T, d_gate_low)
    grad_up = matmul_low(normed2_low.T, d_up_low)
    d_normed2 = lax.psum(
        matmul_low(d_gate_low, full_gate.T) + matmul_low(d_up_low, full_up.T), "head"
    )
    d_resid_norm, grad_gain_ffn = norm_ffn_pull(d_normed2)
    d_resid = cotangent.astype(jnp.float32) + d_resid_norm
    d_attn_low = d_resid.astype(jnp.bfloat16)
    grad_out = matmul_low(mixed_low.T, d_attn_low)
    d_mixed = matmul_low(d_attn_low, full_out.T)
    d_query, d_key, d_value, d_logit = mixer_pull(d_mixed)
    grad_bias_part = jnp.sum(d_logit, axis=0)
    d_query_low = d_query.astype(jnp.bfloat16)
    d_key_low = d_key.astype(jnp.bfloat16)
    d_value_low = d_value.astype(jnp.bfloat16)
    d_logit_low = d_logit.astype(jnp.bfloat16)
    grad_query = matmul_low(normed_low.T, d_query_low)
    grad_key = matmul_low(normed_low.T, d_key_low)
    grad_value = matmul_low(normed_low.T, d_value_low)
    grad_slot = matmul_low(normed_low.T, d_logit_low)
    d_normed_part = (
        matmul_low(d_query_low, full_query.T)
        + matmul_low(d_key_low, full_key.T)
        + matmul_low(d_value_low, full_value.T)
        + matmul_low(d_logit_low, full_slot.T)
    )
    d_normed = lax.psum(d_normed_part.astype(jnp.bfloat16), "head").astype(jnp.float32)
    d_inputs_norm, grad_gain_attn = norm_attn_pull(d_normed)
    grad_inputs = d_resid + d_inputs_norm
    column_grads = (
        lax.psum_scatter(grad_gain_attn, "dp", scatter_dimension=0, tiled=True),
        lax.psum_scatter(grad_gain_ffn, "dp", scatter_dimension=0, tiled=True),
        lax.psum_scatter(grad_query, "dp", scatter_dimension=0, tiled=True),
        lax.psum_scatter(grad_key, "dp", scatter_dimension=0, tiled=True),
        lax.psum_scatter(grad_value, "dp", scatter_dimension=0, tiled=True),
        lax.psum_scatter(grad_slot, "dp", scatter_dimension=0, tiled=True),
        lax.psum_scatter(grad_gate, "dp", scatter_dimension=0, tiled=True),
        lax.psum_scatter(grad_up, "dp", scatter_dimension=0, tiled=True),
    )
    row_grads = (
        lax.psum_scatter(
            grad_out.astype(jnp.bfloat16), "dp", scatter_dimension=1, tiled=True
        ).astype(jnp.float32),
        lax.psum_scatter(
            grad_down.astype(jnp.bfloat16), "dp", scatter_dimension=1, tiled=True
        ).astype(jnp.float32),
    )
    grad_bias = lax.psum(grad_bias_part, "dp")
    return (
        output_low,
        grad_inputs,
        column_grads[0],
        column_grads[2],
        column_grads[3],
        column_grads[4],
        column_grads[5],
        grad_bias,
        row_grads[0],
        column_grads[1],
        column_grads[6],
        column_grads[7],
        row_grads[1],
    )


def solution(mesh):
    in_specs = (
        P("dp", None),
        P("dp"),
        P("dp"),
        P("dp", "head"),
        P("dp", "head"),
        P("dp", "head"),
        P("dp", "head"),
        P("head"),
        P("head", "dp"),
        P("dp"),
        P("dp", "head"),
        P("dp", "head"),
        P("head", "dp"),
        P("dp", None),
    )
    out_specs = (
        P("dp", None),
        P("dp", None),
        P("dp"),
        P("dp", "head"),
        P("dp", "head"),
        P("dp", "head"),
        P("dp", "head"),
        P("head"),
        P("head", "dp"),
        P("dp"),
        P("dp", "head"),
        P("dp", "head"),
        P("head", "dp"),
    )
    return jax.shard_map(
        per_device, mesh=mesh, in_specs=in_specs, out_specs=out_specs, check_vma=False
    )
```

profile of v0, /device:TPU:0, one launch (start us, length us, event | category | flops | bytes accessed | tf_op | source)
XLA Modules:
  0.0 2579.9 jit_solution(14699896438426582661)
XLA Ops:
  13.9 22.4 all-gather
  37.0 31.8 %all_gather.39 = bf16[2048,64]{0,1:T(8,128)(2,1)S(1)} all-gather(bf16[256,64]{0,1:T(8,128)(2,1)S(1)} %copy-done.20), channel_id=1, replica_groups=mesh['dp'=8,'head'=4] {'dp'}, dimensions={0}, use_global_device_ids=true | all-gather | bytes 294912 | tf_op jit(solution)/shard_map/all_gather | solution.py:104
  80.9 34.3 %all-gather.10.cloned.1.call-done = bf16[2048,512]{1,0:T(8,128)(2,1)} async-done(((bf16[256,512]{1,0:T(8,128)(2,1)}), bf16[2048,512]{1,0:T(8,128)(2,1)}) %all-gather.10.cloned.1.call-update) | async-done | bytes 2097168 | tf_op jit(solution)/shard_map/all_gather | solution.py:102
  122.0 43.0 %all-gather.12.cloned.1.call-done = bf16[2048,512]{1,0:T(8,128)(2,1)} async-done(((bf16[256,512]{1,0:T(8,128)(2,1)}), bf16[2048,512]{1,0:T(8,128)(2,1)}) %all-gather.12.cloned.1.call-update) | async-done | bytes 2097168 | tf_op jit(solution)/shard_map/all_gather | solution.py:103
  175.0 216.6 %while.52 = (s32[]{:T(128)}, f32[64,512]{1,0:T(8,128)S(1)}, f32[64,512]{1,0:T(8,128)S(1)}, f32[16,64,512]{2,1,0:T(8,128)}, f32[16,64,512]{2,1,0:T(8,128)}, /*ind...) while((s32[]{:T(128)}, f32[64,512]{1,0:T(8,128)S(1)}, ...), condition=%wide.region_5.6_spmd.clone.clone.clone, body=%wide.region_1.5_spmd.clone.clone.sunk.clone | while | flops 157441920 | bytes 3196303 | solution.py:64
  405.0 18.1 all-gather.1
  423.2 131.2 %all-reduce.9.cloned.1.call-done = f32[1024,2048]{1,0:T(8,128)} async-done(((f32[1024,2048]{1,0:T(8,128)}), f32[1024,2048]{1,0:T(8,128)}) %all-reduce.9.cloned.1.call-update) | async-done | bytes 8388624 | tf_op jit(solution)/shard_map/psum | solution.py:144
  566.3 82.7 %all-gather.18.cloned.1.call-done = bf16[2048,1408]{1,0:T(8,128)(2,1)} async-done(((bf16[256,1408]{1,0:T(8,128)(2,1)}), bf16[2048,1408]{1,0:T(8,128)(2,1)}) %all-gather.18.cloned.1.call-update) | async-done | bytes 5767184 | tf_op jit(solution)/shard_map/all_gather | solution.py:105
  660.8 80.8 %all-gather.20.cloned.1.call-done = bf16[2048,1408]{1,0:T(8,128)(2,1)} async-done(((bf16[256,1408]{1,0:T(8,128)(2,1)}), bf16[2048,1408]{1,0:T(8,128)(2,1)}) %all-gather.20.cloned.1.call-update) | async-done | bytes 5767184 | tf_op jit(solution)/shard_map/all_gather | solution.py:106
  753.3 81.7 %all-gather.22.cloned.1.call-done = bf16[1408,2048]{1,0:T(8,128)(2,1)} async-done(((bf16[1408,256]{1,0:T(8,128)(2,1)}), bf16[1408,2048]{1,0:T(8,128)(2,1)}) %all-gather.22.cloned.1.call-update) | async-done | bytes 5767184 | tf_op jit(solution)/shard_map/all_gather | solution.py:110
  835.0 15.6 multiply_convert_fusion.1
  884.5 137.2 %all-reduce.11.cloned.1.call-done = f32[1024,2048]{1,0:T(8,128)} async-done(((f32[1024,2048]{1,0:T(8,128)}), f32[1024,2048]{1,0:T(8,128)}) %all-reduce.11.cloned.1.call-update) | async-done | bytes 8388624 | tf_op jit(solution)/shard_map/psum | solution.py:178
  1041.6 429.4 %while.51 = (s32[]{:T(128)}, f32[64,512]{1,0:T(8,128)S(1)}, f32[64,512]{1,0:T(8,128)S(1)}, bf16[16,64,512]{2,1,0:T(8,128)(2,1)S(1)}, bf16[16,64,512]{2,1,0:T(8,1...) while((s32[]{:T(128)}, f32[64,512]{1,0:T(8,128)S(1)}, ...), condition=%wide.region_23.24_spmd.clone.clone, body=%wide.region_11.0_spmd.clone.sunk.clone | while | flops 373932032 | bytes 8373975 | solution.py:64
  1569.2 82.9 %all-reduce.13.cloned.1.call-done = (bf16[1024,2048]{1,0:T(8,128)(2,1)}, bf16[1024,2048]{1,0:T(8,128)(2,1)}) async-done(((bf16[1024,2048]{1,0:T(8,128)(2,1)}, bf16[1024,2048]{1,0:T(8,128)(2,1)}), (bf16[1024,2048]{1,0:T(8,128)(2,1)}, bf16[1024,2048]{1,0:T(8,128)(2,1)})) %all-reduce.13.cloned.1.call-update) | async-done | bytes 8388624 | tf_op jit(solution)/shard_map/psum | solution.py:153
  1658.0 38.1 %all-reduce.3 = (f32[2048]{0:T(1024)S(1)}, f32[64]{0:T(128)}, f32[2048]{0:T(1024)S(1)}) all-reduce(f32[2048]{0:T(1024)S(1)} %get-tuple-element.768, f32[64]{0:T(128)S(1)} %neg.61, f32[2048]{0:T(1024)S(1)} %get-tuple-element.766), channel_id=2, replica_groups=mesh['dp'=8,'head'=4] {'dp'}, use_global_device_ids=true, to_apply=%region_27.28.clone | all-reduce | flops 4160 | bytes 33280
  1697.4 27.4 %reduce-scatter.17.cloned.1.call-done = bf16[512,256]{1,0:T(8,128)(2,1)} async-done(((bf16[512,2048]{1,0:T(8,128)(2,1)}), bf16[512,256]{1,0:T(8,128)(2,1)}) %reduce-scatter.17.cloned.1.call-update) | async-done | bytes 262160 | tf_op jit(solution)/shard_map/reduce_scatter | solution.py:216
  1726.5 17.2 fusion.119
  1743.7 94.6 %reduce-scatter.23.cloned.1.call-done = bf16[1408,256]{1,0:T(8,128)(2,1)} async-done(((bf16[1408,2048]{1,0:T(8,128)(2,1)}), bf16[1408,256]{1,0:T(8,128)(2,1)}) %reduce-scatter.23.cloned.1.call-update) | async-done | bytes 720912 | tf_op jit(solution)/shard_map/reduce_scatter | solution.py:219
  1840.6 64.0 %reduce-scatter.15.cloned.1.call-done = f32[256,64]{0,1:T(8,128)} async-done(((f32[2048,64]{0,1:T(8,128)}), f32[256,64]{0,1:T(8,128)}) %reduce-scatter.15.cloned.1.call-update) | async-done | bytes 65552 | tf_op jit(solution)/shard_map/reduce_scatter | solution.py:211
  1904.6 91.5 %reduce-scatter.11.cloned.1.call-done = f32[256,512]{1,0:T(8,128)} async-done(((f32[2048,512]{1,0:T(8,128)}), f32[256,512]{1,0:T(8,128)}) %reduce-scatter.11.cloned.1.call-update) | async-done | bytes 524304 | tf_op jit(solution)/shard_map/reduce_scatter | solution.py:209
  1996.1 92.0 %reduce-scatter.13.cloned.1.call-done = f32[256,512]{1,0:T(8,128)} async-done(((f32[2048,512]{1,0:T(8,128)}), f32[256,512]{1,0:T(8,128)}) %reduce-scatter.13.cloned.1.call-update) | async-done | bytes 524304 | tf_op jit(solution)/shard_map/reduce_scatter | solution.py:210
  2088.1 92.0 %reduce-scatter.9.cloned.1.call-done = f32[256,512]{1,0:T(8,128)} async-done(((f32[2048,512]{1,0:T(8,128)}), f32[256,512]{1,0:T(8,128)}) %reduce-scatter.9.cloned.1.call-update) | async-done | bytes 524304 | tf_op jit(solution)/shard_map/reduce_scatter | solution.py:208
  2180.1 196.5 %reduce-scatter.19.cloned.1.call-done = f32[256,1408]{1,0:T(8,128)} async-done(((f32[2048,1408]{1,0:T(8,128)}), f32[256,1408]{1,0:T(8,128)}) %reduce-scatter.19.cloned.1.call-update) | async-done | bytes 1441808 | tf_op jit(solution)/shard_map/reduce_scatter | solution.py:212
  2376.6 196.0 %reduce-scatter.21.cloned.1.call-done = f32[256,1408]{1,0:T(8,128)} async-done(((f32[2048,1408]{1,0:T(8,128)}), f32[256,1408]{1,0:T(8,128)}) %reduce-scatter.21.cloned.1.call-update) | async-done | bytes 1441808 | tf_op jit(solution)/shard_map/reduce_scatter | solution.py:213
  (1096 shorter events, 887.3 us)
Async XLA Ops:
  7.2 68.2 %all-gather.14.cloned.1.call-start = ((), (), s32[]{:S(2)}) async-start(), calls=%async_computation.10 | async-start | bytes 2359296 | tf_op jit(solution)/shard_map/all_gather | solution.py:101
  7.9 107.3 %all-gather.10.cloned.1.call-start = ((), (), s32[]{:S(2)}) async-start(), calls=%async_computation.8 | async-start | bytes 2359296 | tf_op jit(solution)/shard_map/all_gather | solution.py:102
  8.7 156.3 %all-gather.12.cloned.1.call-start = ((), (), s32[]{:S(2)}) async-start(), calls=%async_computation.9 | async-start | bytes 2359296 | tf_op jit(solution)/shard_map/all_gather | solution.py:103
  9.4 385.8 %all-gather.16.cloned.1.call-start = ((), (), s32[]{:S(2)}) async-start(), calls=%async_computation.11 | async-start | bytes 2359296 | tf_op jit(solution)/shard_map/all_gather | solution.py:109
  10.0 544.4 %all-reduce.9.cloned.1.call-start = ((), (), s32[]{:S(2)}) async-start(), calls=%async_computation.12 | async-start | bytes 16777216 | tf_op jit(solution)/shard_map/psum | solution.py:144
  10.1 58.8 %copy-start.1 = (bf16[1024,2048]{1,0:T(8,128)(2,1)S(1)}, bf16[1024,2048]{1,0:T(8,128)(2,1)}, u32[]{:S(2)}) copy-start(bf16[1024,2048]{1,0:T(8,128)(2,1)} %param.18) | copy-start | bytes 12582916
  13.4 55.5 %copy-start.16 = (f32[1024]{0:T(1024)}, f32[1024]{0:T(1024)S(1)}, u32[]{:S(2)}) copy-start(f32[1024]{0:T(1024)S(1)} %fusion.140) | copy-start | bytes 12292
  402.9 246.1 %all-gather.18.cloned.1.call-start = ((), (), s32[]{:S(2)}) async-start(), calls=%async_computation.13 | async-start | bytes 6488064 | tf_op jit(solution)/shard_map/all_gather | solution.py:105
  403.5 338.2 %all-gather.20.cloned.1.call-start = ((), (), s32[]{:S(2)}) async-start(), calls=%async_computation.14 | async-start | bytes 6488064 | tf_op jit(solution)/shard_map/all_gather | solution.py:106
  404.2 430.8 %all-gather.22.cloned.1.call-start = ((), (), s32[]{:S(2)}) async-start(), calls=%async_computation.15 | async-start | bytes 6488064 | tf_op jit(solution)/shard_map/all_gather | solution.py:110
  405.0 616.8 %all-reduce.11.cloned.1.call-start = ((), (), s32[]{:S(2)}) async-start(), calls=%async_computation.16 | async-start | bytes 16777216 | tf_op jit(solution)/shard_map/psum | solution.py:178
  870.5 781.6 %all-reduce.13.cloned.1.call-start = ((), (), s32[]{:S(2)}) async-start(), calls=%async_computation.25 | async-start | bytes 16777216 | tf_op jit(solution)/shard_map/psum | solution.py:153
  1041.6 431.9 %copy-start.10 = (f32[1024,64]{0,1:T(8,128)S(1)}, f32[1024,64]{0,1:T(8,128)}, u32[]{:S(2)}) copy-start(f32[1024,64]{0,1:T(8,128)} %get-tuple-element.870) | copy-start | bytes 786436
  1498.9 225.8 %reduce-scatter.17.cloned.1.call-start = ((), (), s32[]{:S(2)}) async-start(), calls=%async_computation.21 | async-start | bytes 2359296 | tf_op jit(solution)/shard_map/reduce_scatter | solution.py:216
  1507.2 331.1 %reduce-scatter.23.cloned.1.call-start = ((), (), s32[]{:S(2)}) async-start(), calls=%async_computation.24 | async-start | bytes 6488064 | tf_op jit(solution)/shard_map/reduce_scatter | solution.py:219
  1518.0 386.6 %reduce-scatter.15.cloned.1.call-start = ((), (), s32[]{:S(2)}) async-start(), calls=%async_computation.20 | async-start | bytes 589824 | tf_op jit(solution)/shard_map/reduce_scatter | solution.py:211
  1522.0 474.1 %reduce-scatter.11.cloned.1.call-start = ((), (), s32[]{:S(2)}) async-start(), calls=%async_computation.18 | async-start | bytes 4718592 | tf_op jit(solution)/shard_map/reduce_scatter | solution.py:209
  1528.6 559.5 %reduce-scatter.13.cloned.1.call-start = ((), (), s32[]{:S(2)}) async-start(), calls=%async_computation.19 | async-start | bytes 4718592 | tf_op jit(solution)/shard_map/reduce_scatter | solution.py:210
  1536.3 643.8 %reduce-scatter.9.cloned.1.call-start = ((), (), s32[]{:S(2)}) async-start(), calls=%async_computation.17 | async-start | bytes 4718592 | tf_op jit(solution)/shard_map/reduce_scatter | solution.py:208
  1542.9 833.7 %reduce-scatter.19.cloned.1.call-start = ((), (), s32[]{:S(2)}) async-start(), calls=%async_computation.22 | async-start | bytes 12976128 | tf_op jit(solution)/shard_map/reduce_scatter | solution.py:212
  1555.3 1017.3 %reduce-scatter.21.cloned.1.call-start = ((), (), s32[]{:S(2)}) async-start(), calls=%async_computation.23 | async-start | bytes 12976128 | tf_op jit(solution)/shard_map/reduce_scatter | solution.py:213
  1567.3 84.8 %copy-start.15 = (f32[8,1,256]{2,1,0:T(1,128)S(1)}, f32[8,1,256]{2,1,0:T(1,128)}, u32[]{:S(2)}) copy-start(f32[8,1,256]{2,1,0:T(1,128)} %copy-done.14) | copy-start | bytes 24580
  1567.3 84.8 %copy-start.17 = (f32[1024]{0:T(1024)S(1)}, f32[1024]{0:T(1024)}, u32[]{:S(2)}) copy-start(f32[1024]{0:T(1024)} %copy-done.16) | copy-start | bytes 12292
  1652.1 74.4 %copy-start.19 = (f32[1024]{0:T(1024)S(1)}, f32[1024]{0:T(1024)}, u32[]{:S(2)}) copy-start(f32[1024]{0:T(1024)} %copy-done.18) | copy-start | bytes 12292
  (25 other events, 179.4 us)
Sparse Core Ops, SparseCore 0:
  10.1 54.1 all-gather.13
  66.4 48.7 all-gather.9
  117.4 47.6 all-gather.11
  166.9 48.8 all-gather.15
  403.0 151.3 all-reduce.8
  556.5 92.4 all-gather.17
  651.1 90.4 all-gather.19
  743.7 91.3 all-gather.21
  870.6 151.0 all-reduce.10
  1499.0 153.0 all-reduce.12
  1655.6 69.0 reduce-scatter.16
  1728.3 109.9 reduce-scatter.22
  1842.2 62.3 reduce-scatter.14
  1908.7 87.3 reduce-scatter.10
  2000.1 87.9 reduce-scatter.12
  2092.1 87.9 reduce-scatter.8
  2184.1 192.4 reduce-scatter.18
  2380.6 191.9 reduce-scatter.20
where the time goes:
time: 2590 us; the launch traced here: 2580 us
  waiting for transfers between devices  1530 us (59%)
  matrix products  648 us (25%)
  other arithmetic  155 us (6%)
  local copies, waits for them, and re-layouts  111 us (4%)
  blocking collectives  111 us (4%)
    reduce_scatter x1, waiting for transfers between devices, per_device(): lax.psum_scatter(grad_gate, 'dp', scatter_dimension=0, tiled=True)  197 us
    reduce_scatter x1, waiting for transfers between devices, per_device(): lax.psum_scatter(grad_up, 'dp', scatter_dimension=0, tiled=True)  196 us
    dot_general x24, matrix products, matmul_low(): return jnp.dot(left, right, preferred_element_type=jnp.float32)  191 us
    dot_general x48, matrix products, span_step(): mixing = jnp.einsum('tj,tsj->ts', slot_probs, weighted, precision=highest)  166 us
    psum x1, waiting for transfers between devices, per_device(): lax.psum(matmul_low(d_gate_low, full_gate.T) + matmul_low(d_up_low, full_...  137 us
    psum x1, waiting for transfers between devices, per_device(): resid = rows_in + lax.psum(matmul_low(mixed_low, full_out), 'head')  131 us
    dot_general x32, matrix products, span_step(): jnp.einsum('tsj,ts->tj', weighted, inner_products, precision=highest)  106 us
    reduce_scatter x1, waiting for transfers between devices, per_device(): lax.psum_scatter(grad_down.astype(jnp.bfloat16), 'dp', scatter_dimension=...  94.6 us
  transfers between devices with their start and end apart: 18, of which 16 were waited for; matrix products, arithmetic and copies ran while one was open for 15% of the time, Pallas kernels for 0%

commit v1 on v0

--- a/solution.py
+++ b/solution.py
@@ -7,6 +7,18 @@
 epsilon = 1e-06
 damping = 8.0
 highest = lax.Precision.HIGHEST
+
+
+def collect(value, axis, dim):
+    ways, here = (lax.axis_size(axis), lax.axis_index(axis))
+    grown, reach = (value, 1)
+    while reach < ways:
+        theirs = lax.ppermute(grown, axis, [(d, d ^ reach) for d in range(ways)])
+        mine_first = jnp.concatenate([grown, theirs], axis=dim)
+        theirs_first = jnp.concatenate([theirs, grown], axis=dim)
+        grown = jnp.where(here & reach == 0, mine_first, theirs_first)
+        reach = 2 * reach
+    return grown
 
 
 def norm_rows(values, gain):
@@ -103,7 +115,7 @@
         lax.all_gather(w_value, "dp", axis=0, tiled=True),
         lax.all_gather(w_slot, "dp", axis=0, tiled=True),
         lax.all_gather(w_gate, "dp", axis=0, tiled=True),
-        lax.all_gather(w_up, "dp", axis=0, tiled=True),
+        collect(w_up, "dp", 0),
     )
     row_set = (
         lax.all_gather(w_out, "dp", axis=1, tiled=True),

time: 2590 us -> 2580 us (level)
  waiting for transfers between devices: 1530 us -> 1480 us
    psum x1, waiting for transfers between devices: 131 us -> 82 us  [per_device(): resid = rows_in + lax.psum(matmul_low(mixed_low, full_out), 'head')]
    all_gather x1, waiting for transfers between devices: 80.8 us -> 52.1 us  [per_device(): lax.all_gather(w_up, 'dp', axis=0, tiled=True)]
  transfers between devices with their start and end apart: 18 -> 21, of which waited for: 16 -> 17; matrix products, arithmetic and copies ran while one was open for 15% -> 16% of each run, Pallas kernels for 0% -> 0%
where the time goes in v1:
time: 2580 us; the launch traced here: 2570 us
  waiting for transfers between devices  1480 us (57%)
  matrix products  655 us (25%)
  other arithmetic  162 us (6%)
  blocking collectives  136 us (5%)
  local copies, waits for them, and re-layouts  111 us (4%)
    dot_general x24, matrix products, matmul_low(): return jnp.dot(left, right, preferred_element_type=jnp.float32)  197 us
    reduce_scatter x1, waiting for transfers between devices, per_device(): lax.psum_scatter(grad_gate, 'dp', scatter_dimension=0, tiled=True)  197 us
    reduce_scatter x1, waiting for transfers between devices, per_device(): lax.psum_scatter(grad_up, 'dp', scatter_dimension=0, tiled=True)  196 us
    dot_general x48, matrix products, span_step(): mixing = jnp.einsum('tj,tsj->ts', slot_probs, weighted, precision=highest)  166 us
    psum x1, waiting for transfers between devices, per_device(): lax.psum(matmul_low(d_gate_low, full_gate.T) + matmul_low(d_up_low, full_...  137 us
    dot_general x32, matrix products, span_step(): jnp.einsum('tsj,ts->tj', weighted, inner_products, precision=highest)  106 us
    all_gather x1, waiting for transfers between devices, per_device(): lax.all_gather(w_gate, 'dp', axis=0, tiled=True)  96.9 us
    reduce_scatter x1, waiting for transfers between devices, per_device(): lax.psum_scatter(grad_down.astype(jnp.bfloat16), 'dp', scatter_dimension=...  94.6 us
  transfers between devices with their start and end apart: 21, of which 17 were waited for; matrix products, arithmetic and copies ran while one was open for 16% of the time, Pallas kernels for 0%

profile of v1, /device:TPU:0, one launch (start us, length us, event | category | flops | bytes accessed | tf_op | source)
XLA Modules:
  0.0 2571.7 jit_solution(12144675121116304039)
XLA Ops:
  13.9 22.4 all-gather
  37.0 31.8 %all_gather.38 = bf16[2048,64]{0,1:T(8,128)(2,1)S(1)} all-gather(bf16[256,64]{0,1:T(8,128)(2,1)S(1)} %copy-done.21), channel_id=1, replica_groups=mesh['dp'=8,'head'=4] {'dp'}, dimensions={0}, use_global_device_ids=true | all-gather | bytes 294912 | tf_op jit(solution)/shard_map/all_gather | solution.py:116
  80.9 34.4 %all-gather.10.cloned.1.call-done = bf16[2048,512]{1,0:T(8,128)(2,1)} async-done(((bf16[256,512]{1,0:T(8,128)(2,1)}), bf16[2048,512]{1,0:T(8,128)(2,1)}) %all-gather.10.cloned.1.call-update) | async-done | bytes 2097168 | tf_op jit(solution)/shard_map/all_gather | solution.py:114
  122.1 43.0 %all-gather.12.cloned.1.call-done = bf16[2048,512]{1,0:T(8,128)(2,1)} async-done(((bf16[256,512]{1,0:T(8,128)(2,1)}), bf16[2048,512]{1,0:T(8,128)(2,1)}) %all-gather.12.cloned.1.call-update) | async-done | bytes 2097168 | tf_op jit(solution)/shard_map/all_gather | solution.py:115
  175.1 216.2 %while.52 = (s32[]{:T(128)}, f32[64,512]{1,0:T(8,128)S(1)}, f32[64,512]{1,0:T(8,128)S(1)}, f32[16,64,512]{2,1,0:T(8,128)}, f32[16,64,512]{2,1,0:T(8,128)}, /*ind...) while((s32[]{:T(128)}, f32[64,512]{1,0:T(8,128)S(1)}, ...), condition=%wide.region_5.6_spmd.clone.clone.clone, body=%wide.region_1.5_spmd.clone.clone.sunk.clone | while | flops 157441920 | bytes 3196303 | solution.py:76
  424.3 43.3 %all-gather.1 = bf16[8,1,256]{2,1,0:T(2,128)(2,1)S(1)} all-gather(bf16[1,1,256]{2,1,0:T(2,128)(2,1)S(1)} %reshape.298), channel_id=1, replica_groups=mesh['dp'=8,'head'=4] {'dp'}, dimensions={0}, use_global_device_ids=true | all-gather | bytes 4608 | tf_op jit(solution)/shard_map/all_gather | solution.py:112
  472.1 82.0 %all-reduce.9.cloned.1.call-done = f32[1024,2048]{1,0:T(8,128)} async-done(((f32[1024,2048]{1,0:T(8,128)}), f32[1024,2048]{1,0:T(8,128)}) %all-reduce.9.cloned.1.call-update) | async-done | bytes 8388624 | tf_op jit(solution)/shard_map/psum | solution.py:156
  565.9 96.9 %all-gather.18.cloned.1.call-done = bf16[2048,1408]{1,0:T(8,128)(2,1)} async-done(((bf16[256,1408]{1,0:T(8,128)(2,1)}), bf16[2048,1408]{1,0:T(8,128)(2,1)}) %all-gather.18.cloned.1.call-update) | async-done | bytes 5767184 | tf_op jit(solution)/shard_map/all_gather | solution.py:117
  674.7 82.3 %all-gather.20.cloned.1.call-done = bf16[1408,2048]{1,0:T(8,128)(2,1)} async-done(((bf16[1408,256]{1,0:T(8,128)(2,1)}), bf16[1408,2048]{1,0:T(8,128)(2,1)}) %all-gather.20.cloned.1.call-update) | async-done | bytes 5767184 | tf_op jit(solution)/shard_map/all_gather | solution.py:122
  768.8 17.3 multiply_convert_fusion.1
  797.6 52.1 %all-gather.22.cloned.1.call-done = bf16[2048,1408]{1,0:T(8,128)(2,1)} async-done(((bf16[256,1408]{1,0:T(8,128)(2,1)}), bf16[2048,1408]{1,0:T(8,128)(2,1)}) %all-gather.22.cloned.1.call-update) | async-done | bytes 5767184 | tf_op jit(solution)/shard_map/all_gather | solution.py:175
  876.6 137.5 %all-reduce.11.cloned.1.call-done = f32[1024,2048]{1,0:T(8,128)} async-done(((f32[1024,2048]{1,0:T(8,128)}), f32[1024,2048]{1,0:T(8,128)}) %all-reduce.11.cloned.1.call-update) | async-done | bytes 8388624 | tf_op jit(solution)/shard_map/psum | solution.py:190
  1033.9 429.3 %while.51 = (s32[]{:T(128)}, f32[64,512]{1,0:T(8,128)S(1)}, f32[64,512]{1,0:T(8,128)S(1)}, bf16[16,64,512]{2,1,0:T(8,128)(2,1)S(1)}, bf16[16,64,512]{2,1,0:T(8,1...) while((s32[]{:T(128)}, f32[64,512]{1,0:T(8,128)S(1)}, ...), condition=%wide.region_23.24_spmd.clone.clone, body=%wide.region_11.23_spmd.clone.sunk.clone | while | flops 373932032 | bytes 8373975 | solution.py:76
  1561.4 82.7 %all-reduce.13.cloned.1.call-done = (bf16[1024,2048]{1,0:T(8,128)(2,1)}, bf16[1024,2048]{1,0:T(8,128)(2,1)}) async-done(((bf16[1024,2048]{1,0:T(8,128)(2,1)}, bf16[1024,2048]{1,0:T(8,128)(2,1)}), (bf16[1024,2048]{1,0:T(8,128)(2,1)}, bf16[1024,2048]{1,0:T(8,128)(2,1)})) %all-reduce.13.cloned.1.call-update) | async-done | bytes 8388624 | tf_op jit(solution)/shard_map/psum | solution.py:165
  1650.0 38.1 %all-reduce.3 = (f32[2048]{0:T(1024)S(1)}, f32[64]{0:T(128)}, f32[2048]{0:T(1024)S(1)}) all-reduce(f32[2048]{0:T(1024)S(1)} %get-tuple-element.768, f32[64]{0:T(128)S(1)} %neg.61, f32[2048]{0:T(1024)S(1)} %get-tuple-element.766), channel_id=2, replica_groups=mesh['dp'=8,'head'=4] {'dp'}, use_global_device_ids=true, to_apply=%region_27.28.clone | all-reduce | flops 4160 | bytes 33280
  1689.4 27.4 %reduce-scatter.17.cloned.1.call-done = bf16[512,256]{1,0:T(8,128)(2,1)} async-done(((bf16[512,2048]{1,0:T(8,128)(2,1)}), bf16[512,256]{1,0:T(8,128)(2,1)}) %reduce-scatter.17.cloned.1.call-update) | async-done | bytes 262160 | tf_op jit(solution)/shard_map/reduce_scatter | solution.py:228
  1718.6 17.2 fusion.119
  1735.7 94.6 %reduce-scatter.23.cloned.1.call-done = bf16[1408,256]{1,0:T(8,128)(2,1)} async-done(((bf16[1408,2048]{1,0:T(8,128)(2,1)}), bf16[1408,256]{1,0:T(8,128)(2,1)}) %reduce-scatter.23.cloned.1.call-update) | async-done | bytes 720912 | tf_op jit(solution)/shard_map/reduce_scatter | solution.py:231
  1832.7 64.0 %reduce-scatter.15.cloned.1.call-done = f32[256,64]{0,1:T(8,128)} async-done(((f32[2048,64]{0,1:T(8,128)}), f32[256,64]{0,1:T(8,128)}) %reduce-scatter.15.cloned.1.call-update) | async-done | bytes 65552 | tf_op jit(solution)/shard_map/reduce_scatter | solution.py:223
  1896.7 91.5 %reduce-scatter.11.cloned.1.call-done = f32[256,512]{1,0:T(8,128)} async-done(((f32[2048,512]{1,0:T(8,128)}), f32[256,512]{1,0:T(8,128)}) %reduce-scatter.11.cloned.1.call-update) | async-done | bytes 524304 | tf_op jit(solution)/shard_map/reduce_scatter | solution.py:221
  1988.1 92.0 %reduce-scatter.13.cloned.1.call-done = f32[256,512]{1,0:T(8,128)} async-done(((f32[2048,512]{1,0:T(8,128)}), f32[256,512]{1,0:T(8,128)}) %reduce-scatter.13.cloned.1.call-update) | async-done | bytes 524304 | tf_op jit(solution)/shard_map/reduce_scatter | solution.py:222
  2080.1 92.0 %reduce-scatter.9.cloned.1.call-done = f32[256,512]{1,0:T(8,128)} async-done(((f32[2048,512]{1,0:T(8,128)}), f32[256,512]{1,0:T(8,128)}) %reduce-scatter.9.cloned.1.call-update) | async-done | bytes 524304 | tf_op jit(solution)/shard_map/reduce_scatter | solution.py:220
  2172.2 196.5 %reduce-scatter.19.cloned.1.call-done = f32[256,1408]{1,0:T(8,128)} async-done(((f32[2048,1408]{1,0:T(8,128)}), f32[256,1408]{1,0:T(8,128)}) %reduce-scatter.19.cloned.1.call-update) | async-done | bytes 1441808 | tf_op jit(solution)/shard_map/reduce_scatter | solution.py:224
  2368.7 196.0 %reduce-scatter.21.cloned.1.call-done = f32[256,1408]{1,0:T(8,128)} async-done(((f32[2048,1408]{1,0:T(8,128)}), f32[256,1408]{1,0:T(8,128)}) %reduce-scatter.21.cloned.1.call-update) | async-done | bytes 1441808 | tf_op jit(solution)/shard_map/reduce_scatter | solution.py:225
  (1100 shorter events, 916.1 us)
Async XLA Ops:
  7.2 68.2 %all-gather.14.cloned.1.call-start = ((), (), s32[]{:S(2)}) async-start(), calls=%async_computation.10 | async-start | bytes 2359296 | tf_op jit(solution)/shard_map/all_gather | solution.py:113
  7.9 107.3 %all-gather.10.cloned.1.call-start = ((), (), s32[]{:S(2)}) async-start(), calls=%async_computation.8 | async-start | bytes 2359296 | tf_op jit(solution)/shard_map/all_gather | solution.py:114
  8.7 156.4 %all-gather.12.cloned.1.call-start = ((), (), s32[]{:S(2)}) async-start(), calls=%async_computation.9 | async-start | bytes 2359296 | tf_op jit(solution)/shard_map/all_gather | solution.py:115
  9.4 385.4 %all-gather.16.cloned.1.call-start = ((), (), s32[]{:S(2)}) async-start(), calls=%async_computation.11 | async-start | bytes 2359296 | tf_op jit(solution)/shard_map/all_gather | solution.py:121
  10.0 544.1 %all-reduce.9.cloned.1.call-start = ((), (), s32[]{:S(2)}) async-start(), calls=%async_computation.12 | async-start | bytes 16777216 | tf_op jit(solution)/shard_map/psum | solution.py:156
  402.5 260.2 %all-gather.18.cloned.1.call-start = ((), (), s32[]{:S(2)}) async-start(), calls=%async_computation.13 | async-start | bytes 6488064 | tf_op jit(solution)/shard_map/all_gather | solution.py:117
  403.1 353.9 %all-gather.20.cloned.1.call-start = ((), (), s32[]{:S(2)}) async-start(), calls=%async_computation.14 | async-start | bytes 6488064 | tf_op jit(solution)/shard_map/all_gather | solution.py:122
  403.9 445.8 %all-gather.22.cloned.1.call-start = ((), (), s32[]{:S(2)}) async-start(), calls=%async_computation.15 | async-start | bytes 6488064 | tf_op jit(solution)/shard_map/all_gather | solution.py:175
  403.9 16.2 collective-permute-start
  421.8 45.9 %collective-permute-start.1 = (bf16[512,1408]{1,0:T(8,128)(2,1)S(1)}, bf16[512,1408]{1,0:T(8,128)(2,1)}, u32[]{:S(2)}, u32[]{:S(2)}) collective-permute-start(bf16[512,1408]{1,0:T(8,128)(2,1)S(1)} %maximum_select_fusion.3), channel_id=1, source_target_pairs={{0,8},{4,12},{8,0},{12,4},{16,24},{20,28},{24,16},{28,20},{1,9},{5... | collective-permute-start | bytes 4325384 | tf_op jit(solution)/shard_map/ppermute | solution.py:16
  424.3 589.8 %all-reduce.11.cloned.1.call-start = ((), (), s32[]{:S(2)}) async-start(), calls=%async_computation.16 | async-start | bytes 16777216 | tf_op jit(solution)/shard_map/psum | solution.py:190
  472.1 296.7 %collective-permute-start.2 = (bf16[1024,1408]{1,0:T(8,128)(2,1)}, bf16[1024,1408]{1,0:T(8,128)(2,1)}, u32[]{:S(2)}, u32[]{:S(2)}) collective-permute-start(bf16[1024,1408]{1,0:T(8,128)(2,1)} %maximum_select_fusion.2), channel_id=1, source_target_pairs={{0,16},{4,20},{8,24},{12,28},{16,0},{20,4},{24,8},{28,12},{1,17},{... | collective-permute-start | bytes 8650760 | tf_op jit(solution)/shard_map/ppermute | solution.py:16
  862.8 781.3 %all-reduce.13.cloned.1.call-start = ((), (), s32[]{:S(2)}) async-start(), calls=%async_computation.25 | async-start | bytes 16777216 | tf_op jit(solution)/shard_map/psum | solution.py:165
  1033.9 431.8 %copy-start.11 = (f32[1024,64]{0,1:T(8,128)S(1)}, f32[1024,64]{0,1:T(8,128)}, u32[]{:S(2)}) copy-start(f32[1024,64]{0,1:T(8,128)} %get-tuple-element.870) | copy-start | bytes 786436
  1491.0 225.8 %reduce-scatter.17.cloned.1.call-start = ((), (), s32[]{:S(2)}) async-start(), calls=%async_computation.21 | async-start | bytes 2359296 | tf_op jit(solution)/shard_map/reduce_scatter | solution.py:228
  1499.3 331.1 %reduce-scatter.23.cloned.1.call-start = ((), (), s32[]{:S(2)}) async-start(), calls=%async_computation.24 | async-start | bytes 6488064 | tf_op jit(solution)/shard_map/reduce_scatter | solution.py:231
  1510.3 386.4 %reduce-scatter.15.cloned.1.call-start = ((), (), s32[]{:S(2)}) async-start(), calls=%async_computation.20 | async-start | bytes 589824 | tf_op jit(solution)/shard_map/reduce_scatter | solution.py:223
  1514.3 473.8 %reduce-scatter.11.cloned.1.call-start = ((), (), s32[]{:S(2)}) async-start(), calls=%async_computation.18 | async-start | bytes 4718592 | tf_op jit(solution)/shard_map/reduce_scatter | solution.py:221
  1520.9 559.3 %reduce-scatter.13.cloned.1.call-start = ((), (), s32[]{:S(2)}) async-start(), calls=%async_computation.19 | async-start | bytes 4718592 | tf_op jit(solution)/shard_map/reduce_scatter | solution.py:222
  1528.6 643.6 %reduce-scatter.9.cloned.1.call-start = ((), (), s32[]{:S(2)}) async-start(), calls=%async_computation.17 | async-start | bytes 4718592 | tf_op jit(solution)/shard_map/reduce_scatter | solution.py:220
  1535.2 833.5 %reduce-scatter.19.cloned.1.call-start = ((), (), s32[]{:S(2)}) async-start(), calls=%async_computation.22 | async-start | bytes 12976128 | tf_op jit(solution)/shard_map/reduce_scatter | solution.py:224
  1547.5 1017.2 %reduce-scatter.21.cloned.1.call-start = ((), (), s32[]{:S(2)}) async-start(), calls=%async_computation.23 | async-start | bytes 12976128 | tf_op jit(solution)/shard_map/reduce_scatter | solution.py:225
  1559.5 84.6 %copy-start.16 = (f32[8,1,256]{2,1,0:T(1,128)S(1)}, f32[8,1,256]{2,1,0:T(1,128)}, u32[]{:S(2)}) copy-start(f32[8,1,256]{2,1,0:T(1,128)} %copy-done.15) | copy-start | bytes 24580
  1559.5 84.6 %copy-start.18 = (f32[1024]{0:T(1024)S(1)}, f32[1024]{0:T(1024)}, u32[]{:S(2)}) copy-start(f32[1024]{0:T(1024)} %copy-done.17) | copy-start | bytes 12292
  (26 other events, 356.3 us)
Sparse Core Ops, SparseCore 0:
  10.1 54.1 all-gather.13
  66.4 48.7 all-gather.9
  117.4 47.6 all-gather.11
  167.0 48.8 all-gather.15
  402.6 151.4 all-reduce.8
  556.1 106.5 all-gather.17
  664.8 92.1 all-gather.19
  759.2 90.4 all-gather.21
  863.0 151.0 all-reduce.10
  1491.1 152.9 all-reduce.12
  1647.7 69.0 reduce-scatter.16
  1720.3 109.9 reduce-scatter.22
  1834.3 62.3 reduce-scatter.14
  1900.7 87.3 reduce-scatter.10
  1992.2 87.9 reduce-scatter.12
  2084.2 87.9 reduce-scatter.8
  2176.2 192.4 reduce-scatter.18
  2372.7 191.9 reduce-scatter.20
